TPU v7x, 32 devices: a whole 2x2x4 slice. The times are simulated.
32 devices in a mesh: ka: 4 (over y, x), gy: 8 (over z, core).
Axes of the slice: x: 2, y: 2, z: 4, core: 2. Of those that a mesh axis runs over, the one named last changes fastest.
Arguments:
- driving_coefficients: float32 [2, 32768, 2, 192], P(None, 'ka', None, 'gy'), may hold values from -6 to 6
Outputs:
- velocity_coefficients: float32 [2, 32768, 2, 192], P(None, 'ka', None, 'gy')
- spectrum: float32 [2, 192], P(None, 'gy')
All inputs are finite; a program needn't handle non-finite values.
Results may differ from a plain program's by a relative error of at most 0.0003.
Values sent between devices are 32-bit elements.
A program may use at most 128 MiB of HBM per device.

v0:
```python
import jax
import jax.numpy as jnp
from jax import lax
from jax.sharding import PartitionSpec as P

MODES_Z = 512
NCH = 384


viscous_rate = 400.0
wave_x = 1.0
wave_z = 2.0


def padded_2(block, sides, width, periodic):
    for axis, dim in sides:
        count = lax.axis_size(axis)
        forward = [(i, i + 1) for i in range(count - 1)]
        if periodic:
            forward.append((count - 1, 0))
        backward = [(target, source) for source, target in forward]
        low = lax.ppermute(
            lax.slice_in_dim(block, block.shape[dim] - width, None, axis=dim), axis, forward
        )
        high = lax.ppermute(lax.slice_in_dim(block, 0, width, axis=dim), axis, backward)
        block = jnp.concatenate([low, block, high], axis=dim)
    return block


def carried_in(x, axis, combine, identity, reverse):
    count, place = lax.axis_size(axis), lax.axis_index(axis)
    everything = jax.tree.map(lambda part: lax.all_gather(part, axis), x)
    start = jax.tree.map(
        lambda part, zero: jnp.broadcast_to(jnp.asarray(zero, part.dtype), part.shape), x, identity
    )

    def lap(k, before):
        at = count - 1 - k if reverse else k
        reached = at > place if reverse else at < place
        new = combine(before, jax.tree.map(lambda part: part[at], everything))
        return jax.tree.map(lambda a, b: jnp.where(reached, a, b), new, before)

    return lax.fori_loop(0, count, lap, start)


def helm_shift(pair_ids):
    col_x = pair_ids // MODES_Z
    col_z = pair_ids % MODES_Z
    signed = jnp.where(col_z < MODES_Z // 2, col_z, col_z - MODES_Z)
    wave_kx = wave_x * col_x.astype(jnp.float32)
    wave_kz = wave_z * signed.astype(jnp.float32)
    return wave_kx * wave_kx + wave_kz * wave_kz + viscous_rate


def row_weights(glob_rows):
    parity = jnp.arange(2, dtype=jnp.int32)
    order_int = 2 * glob_rows[None, :] + parity[:, None]
    top_row = jnp.broadcast_to((glob_rows == 0)[None, :], order_int.shape)
    degree = jnp.where(top_row, 4, order_int).astype(jnp.float32)
    lower_w = jnp.where(order_int == 2, 2.0, 1.0) / (4.0 * degree * (degree - 1.0))
    middle_w = jnp.where(order_int <= NCH - 3, 1.0, 0.0) / (2.0 * (degree * degree - 1.0))
    upper_w = jnp.where(order_int + 2 <= NCH - 3, 1.0, 0.0) / (4.0 * degree * (degree + 1.0))
    lower_w = jnp.where(top_row, 0.0, lower_w)
    middle_w = jnp.where(top_row, 0.0, middle_w)
    upper_w = jnp.where(top_row, 0.0, upper_w)
    return (top_row, lower_w, middle_w, upper_w)


def system(shift_sq, glob_rows, padded):
    top_row, lower_w, middle_w, upper_w = row_weights(glob_rows)
    shift_col = shift_sq[:, None, None]
    lower_band = shift_col * lower_w
    diag_band = jnp.where(top_row, 1.0, -(1.0 + shift_col * middle_w))
    above_diagonal_entries = shift_col * upper_w
    source = -viscous_rate * (
        lower_w * padded[..., :-2] - middle_w * padded[..., 1:-1] + upper_w * padded[..., 2:]
    )
    single_forcing_vector = jnp.broadcast_to(jnp.where(top_row, 1.0, 0.0), lower_band.shape).astype(
        source.dtype
    )
    sources = jnp.concatenate([source, single_forcing_vector[None]], axis=0)
    return (lower_band, diag_band, above_diagonal_entries, sources)


def stacked_rows(lower_band, diag_band, above_diagonal_entries, sources):
    return (
        jnp.moveaxis(lower_band, -1, 0),
        jnp.moveaxis(diag_band, -1, 0),
        jnp.moveaxis(above_diagonal_entries, -1, 0),
        jnp.moveaxis(sources, -1, 0),
    )


def eliminate(stacked, factor_in, offset_in):

    def advance(running, row_stack):
        factor, offset = running
        row_low, row_diag, row_high, row_src = row_stack
        pivot_row = row_diag - row_low * factor
        updated_multiplier = row_high / pivot_row
        offset_new = (row_src - row_low * offset) / pivot_row
        return ((updated_multiplier, offset_new), (updated_multiplier, offset_new))

    return lax.scan(advance, (factor_in, offset_in), stacked)[1]


def substitute(factors, starting_positions, start_in):

    def retreat(running, row_pair):
        line_multiplier, row_offset = row_pair
        result = row_offset - line_multiplier * running
        return (result, result)

    return jnp.moveaxis(
        lax.scan(retreat, start_in, (factors, starting_positions), reverse=True)[1], 0, -1
    )


def closing(columns, sum_free, sum_unit):
    wall_coef = -sum_free / sum_unit
    return columns[:2] + wall_coef[..., None] * columns[2][None]


def compose(earlier, later):
    new_xx = later[0] * earlier[0] + later[1] * earlier[2]
    new_xz = later[0] * earlier[1] + later[1] * earlier[3]
    new_zx = later[2] * earlier[0] + later[3] * earlier[2]
    new_zz = later[2] * earlier[1] + later[3] * earlier[3]
    decay = later[4] * earlier[4]
    from_x = later[4] * earlier[5] + later[5] * earlier[0] + later[6] * earlier[2]
    from_z = later[4] * earlier[6] + later[5] * earlier[1] + later[6] * earlier[3]
    largest = jnp.maximum(
        jnp.maximum(jnp.abs(new_xx), jnp.abs(new_xz)), jnp.maximum(jnp.abs(new_zx), jnp.abs(new_zz))
    )
    return tuple(
        (member / largest for member in (new_xx, new_xz, new_zx, new_zz, decay, from_x, from_z))
    )


def chain(earlier, later):
    return (later[0] * earlier[0], later[0] * earlier[1] + later[1])


def per_device(driving_coefficients):
    pair_count = driving_coefficients.shape[1]
    row_count = driving_coefficients.shape[3]
    pair_ids = lax.axis_index("ka") * pair_count + jnp.arange(pair_count, dtype=jnp.int32)
    glob_rows = lax.axis_index("gy") * row_count + jnp.arange(row_count, dtype=jnp.int32)
    padded = padded_2(driving_coefficients, (("gy", 3),), 1, False)
    stacked = stacked_rows(*system(helm_shift(pair_ids), glob_rows, padded))
    ones_p = jnp.ones((pair_count, 2), jnp.float32)
    zeros_p = jnp.zeros((pair_count, 2), jnp.float32)
    zeros_v = jnp.zeros((3, pair_count, 2), jnp.float32)

    def absorb(running, row_stack):
        row_low, row_diag, row_high, row_src = row_stack
        single = (
            jnp.zeros_like(row_low),
            row_high,
            -row_low,
            row_diag,
            -row_low,
            jnp.zeros_like(row_src),
            row_src,
        )
        return (compose(running, single), None)

    brief_report = lax.scan(
        absorb, (ones_p, zeros_p, zeros_p, ones_p, ones_p, zeros_v, zeros_v), stacked
    )[0]
    m_xx, m_xz, m_zx, m_zz, decay, from_x, from_z = brief_report
    entering = carried_in(
        (m_xx, m_xz, m_zx, m_zz, decay, from_x, from_z),
        "gy",
        compose,
        (ones_p, zeros_p, zeros_p, ones_p, ones_p, zeros_v, zeros_v),
        False,
    )
    factor_in = entering[1] / entering[3]
    offset_in = entering[6] / entering[3]
    factors, starting_positions = eliminate(stacked, factor_in, offset_in)

    def fold_back(running, row_pair):
        gain_now, shift_now = running
        line_multiplier, row_offset = row_pair
        return ((-line_multiplier * gain_now, row_offset - line_multiplier * shift_now), None)

    block_gain, block_shift = lax.scan(
        fold_back, (ones_p, zeros_v), (factors, starting_positions), reverse=True
    )[0]
    incoming = carried_in((block_gain, block_shift), "gy", chain, (ones_p, zeros_v), True)
    columns = substitute(factors, starting_positions, incoming[1])
    totals = lax.psum((jnp.sum(columns[:2], axis=-1), jnp.sum(columns[2], axis=-1)), "gy")
    velocity_coefficients = closing(columns, totals[0], totals[1])
    squares = lax.psum(jnp.sum(velocity_coefficients * velocity_coefficients, axis=(0, 1)), "ka")
    spectrum = squares / (2.0 * pair_count * lax.axis_size("ka"))
    return (velocity_coefficients, spectrum)


def solution(mesh):
    in_specs = (P(None, "ka", None, "gy"),)
    out_specs = (P(None, "ka", None, "gy"), P(None, "gy"))
    return jax.shard_map(
        per_device, mesh=mesh, in_specs=in_specs, out_specs=out_specs, check_vma=False
    )
```

profile of v0, /device:TPU:0, one launch (start us, length us, event | category | flops | bytes accessed | tf_op | source)
XLA Modules:
  0.0 624.4 jit_solution(7639805329509579025)
XLA Ops:
  7.2 4.3 copy.9
  12.3 3.1 collective-permute-start
  16.8 4.0 negate_select_fusion
  21.6 6.5 %fusion.23 = f32[2,8192,2,24]{1,2,0,3:T(2,128)S(1)} fusion(f32[2,8192,2,1]{1,2,0,3:T(2,128)} %collective-permute-done.1, f32[2,8192,2,24]{1,2,0,3:T(2,128)S(1)} %copy.9, f32[2,8192,2,1]{1,2,0,3:T(2,128)} %collective-permute-done, f32[2,24]{0,1:T(8,128)} %get-tuple-element.972, f32[2,24]{0,1:T(8,128)} %get-tuple-element.973, f32[2,24]{0,1:T(8,128)S(1)} %get-tuple-element.971), kind=kLoop, calls=%fused_computation.75 | loop fusion | flops 6291456 | bytes 6554176 | tf_op jit(solution)/shard_map/mul | solution.py:75
  28.6 4.5 maximum_bitcast_fusion
  33.1 63.1 %while.112 = (s32[]{:T(128)}, f32[8192,2]{0,1:T(2,128)S(1)}, f32[8192,2]{0,1:T(2,128)S(1)}, f32[8192,2]{0,1:T(2,128)S(1)}, f32[8192,2]{0,1:T(2,128)S(1)}, /*inde...) while((s32[]{:T(128)}, f32[8192,2]{0,1:T(2,128)S(1)}, ...), condition=%wide.region_1.2_spmd.clone, body=%wide.region_0.1_spmd.clone.sunk | while | flops 1097731 | bytes 3211416 | solution.py:168
  97.8 18.9 %all-gather = f32[65536,2]{0,1:T(2,128)S(1)} all-gather(f32[8192,2]{0,1:T(2,128)S(1)} %get-tuple-element.688), channel_id=2, replica_groups=mesh['ka'=4,'gy'=8] {'gy'}, dimensions={0}, use_global_device_ids=true | all-gather | bytes 589824 | tf_op jit(solution)/shard_map/all_gather | solution.py:32
  116.7 17.7 %all-gather.1 = f32[65536,2]{0,1:T(2,128)} all-gather(f32[8192,2]{0,1:T(2,128)S(1)} %get-tuple-element.689), channel_id=3, replica_groups=mesh['ka'=4,'gy'=8] {'gy'}, dimensions={0}, use_global_device_ids=true | all-gather | bytes 589824 | tf_op jit(solution)/shard_map/all_gather | solution.py:32
  134.4 17.8 %all-gather.2 = f32[65536,2]{0,1:T(2,128)S(1)} all-gather(f32[8192,2]{0,1:T(2,128)S(1)} %get-tuple-element.690), channel_id=4, replica_groups=mesh['ka'=4,'gy'=8] {'gy'}, dimensions={0}, use_global_device_ids=true | all-gather | bytes 589824 | tf_op jit(solution)/shard_map/all_gather | solution.py:32
  152.2 15.0 %all-gather.3 = f32[65536,2]{0,1:T(2,128)S(1)} all-gather(f32[8192,2]{0,1:T(2,128)S(1)} %get-tuple-element.691), channel_id=5, replica_groups=mesh['ka'=4,'gy'=8] {'gy'}, dimensions={0}, use_global_device_ids=true | all-gather | bytes 589824 | tf_op jit(solution)/shard_map/all_gather | solution.py:32
  167.2 14.7 %all-gather.4 = f32[65536,2]{0,1:T(2,128)S(1)} all-gather(f32[8192,2]{0,1:T(2,128)S(1)} %get-tuple-element.692), channel_id=6, replica_groups=mesh['ka'=4,'gy'=8] {'gy'}, dimensions={0}, use_global_device_ids=true | all-gather | bytes 589824 | tf_op jit(solution)/shard_map/all_gather | solution.py:32
  181.9 21.2 %while.113 = (s32[]{:T(128)}, f32[8192,2]{0,1:T(2,128)S(1)}, f32[8192,2]{0,1:T(2,128)S(1)}, f32[8192,2]{0,1:T(2,128)S(1)}, f32[8192,2]{0,1:T(2,128)S(1)}, /*inde...) while((s32[]{:T(128)}, f32[8192,2]{0,1:T(2,128)S(1)}, ...), condition=%wide.region_3.4_spmd.clone, body=%wide.region_2.3_spmd.clone.sunk | while | flops 933892 | bytes 3211454 | solution.py:43
  203.2 81.8 %while.110 = (s32[]{:T(128)}, f32[8192,2]{0,1:T(2,128)S(1)}, f32[3,8192,2]{1,2,0:T(2,128)S(1)}, f32[24,8192,2]{1,2,0:T(2,128)}, f32[24,3,8192,2]{2,3,1,0:T(2,128...) while((s32[]{:T(128)}, f32[8192,2]{0,1:T(2,128)S(1)}, ...), condition=%wide.region_5.6_spmd, body=%wide.region_4.5_spmd.sunk | while | flops 196610 | bytes 1442917 | solution.py:104
  204.9 1.8 bitcast_dynamic-update-slice_fusion.5
  208.3 1.8 bitcast_dynamic-update-slice_fusion.5
  211.7 1.8 bitcast_dynamic-update-slice_fusion.5
  215.1 1.8 bitcast_dynamic-update-slice_fusion.5
  218.5 1.8 bitcast_dynamic-update-slice_fusion.5
  225.3 1.8 bitcast_dynamic-update-slice_fusion.5
  232.1 1.8 bitcast_dynamic-update-slice_fusion.5
  238.9 1.8 bitcast_dynamic-update-slice_fusion.5
  242.3 1.8 bitcast_dynamic-update-slice_fusion.5
  252.5 1.8 bitcast_dynamic-update-slice_fusion.5
  255.9 1.8 bitcast_dynamic-update-slice_fusion.5
  259.4 1.8 bitcast_dynamic-update-slice_fusion.5
  262.8 1.8 bitcast_dynamic-update-slice_fusion.5
  273.0 1.8 bitcast_dynamic-update-slice_fusion.5
  276.4 1.8 bitcast_dynamic-update-slice_fusion.5
  283.2 1.8 bitcast_dynamic-update-slice_fusion.5
  285.0 51.0 %while.114 = (s32[]{:T(128)}, f32[8192,2]{0,1:T(2,128)S(1)}, f32[3,8192,2]{1,2,0:T(2,128)S(1)}, f32[24,8192,2]{1,2,0:T(2,128)}, f32[24,3,8192,2]{2,3,1,0:T(2,128)}, /*index=5*/s32[]{:T(128)}, s32[]{:T(128)}, s32[]{:T(128)}) while((s32[]{:T(128)}, f32[8192,2]{0,1:T(2,128)S(1)}, f32[3,8192,2]{1,2,0:T(2,128)S(1)}, ...), condition=%wide.region_7.8_spmd.clone, body=%wide.region_6.7_spmd.clone.sunk | while | flops 196612 | bytes 917620 | solution.py:188
  336.8 16.0 %all-gather.7 = f32[65536,2]{0,1:T(2,128)S(1)} all-gather(f32[8192,2]{0,1:T(2,128)S(1)} %get-tuple-element.700), channel_id=9, replica_groups=mesh['ka'=4,'gy'=8] {'gy'}, dimensions={0}, use_global_device_ids=true | all-gather | bytes 589824 | tf_op jit(solution)/shard_map/all_gather | solution.py:32
  352.8 11.2 %all-gather.17.cloned.1.call-done = f32[24,8192,2]{1,2,0:T(2,128)} async-done(((f32[3,8192,2]{1,2,0:T(2,128)}), f32[24,8192,2]{1,2,0:T(2,128)}) %all-gather.17.cloned.1.call-update) | async-done | bytes 1572880 | tf_op jit(solution)/shard_map/all_gather | solution.py:32
  364.0 9.1 %while.115 = (s32[]{:T(128)}, f32[3,8192,2]{1,2,0:T(2,128)S(1)}, s32[]{:T(128)}, f32[8,8192,2]{1,2,0:T(2,128)S(1)}, f32[8,3,8192,2]{2,3,1,0:T(2,128)}, /*index=5*/s32[]{:T(128)}, s32[]{:T(128)}, s32[]{:T(128)}, s32[]{:T(128)}) while((s32[]{:T(128)}, f32[3,8192,2]{1,2,0:T(2,128)S(1)}, s32[]{:T(128)}, f32[8,8192,2]{1,2,0:T(2,128)S(1)}, ...), condition=%wide.region_9.10_spmd.clone, body=%wide.region_8.9_spmd.clone.sunk | while | flops 196616 | bytes 786599 | solution.py:43
  373.0 2.7 broadcast.575.clone
  375.7 166.9 %while.111 = (s32[]{:T(128)}, f32[3,8192,2]{1,2,0:T(2,128)S(1)}, f32[24,3,8192,2]{2,0,3,1:T(8,128)}, f32[24,3,8192,2]{2,3,1,0:T(2,128)}, f32[24,8192,2]{1,2,0:T(2,128)}, /*index=5*/s32[]{:T(128)}, s32[]{:T(128)}, s32[]{:T(128)}) while((s32[]{:T(128)}, f32[3,8192,2]{1,2,0:T(2,128)S(1)}, f32[24,3,8192,2]{2,0,3,1:T(8,128)}, ...), condition=%wide.region_11.12_spmd, body=%wide.region_10.11_spmd.sunk | while | flops 98307 | bytes 1572973 | solution.py:115
  377.8 4.8 dynamic_update_slice.24
  384.8 4.8 dynamic_update_slice.24
  391.7 4.8 dynamic_update_slice.24
  398.7 4.8 dynamic_update_slice.24
  405.6 4.8 dynamic_update_slice.24
  412.6 4.8 dynamic_update_slice.24
  419.5 4.8 dynamic_update_slice.24
  426.5 4.8 dynamic_update_slice.24
  433.4 4.8 dynamic_update_slice.24
  440.4 4.8 dynamic_update_slice.24
  447.3 4.8 dynamic_update_slice.24
  454.3 4.8 dynamic_update_slice.24
  461.2 4.8 dynamic_update_slice.24
  468.2 4.8 dynamic_update_slice.24
  475.1 4.8 dynamic_update_slice.24
  482.1 4.8 dynamic_update_slice.24
  489.0 4.8 dynamic_update_slice.24
  496.0 4.8 dynamic_update_slice.24
  503.0 4.8 dynamic_update_slice.24
  509.9 4.8 dynamic_update_slice.24
  516.9 4.8 dynamic_update_slice.24
  523.8 4.8 dynamic_update_slice.24
  530.8 4.8 dynamic_update_slice.24
  537.8 4.8 dynamic_update_slice.24
  542.6 2.3 slice_reduce_fusion.1
  544.9 3.0 slice_reduce_fusion
  547.9 54.7 %all-reduce.3.cloned.1.call-done = (f32[2,8192,2]{1,2,0:T(2,128)}, f32[8192,2]{0,1:T(2,128)}) async-done(((f32[2,8192,2]{1,2,0:T(2,128)}, f32[8192,2]{0,1:T(2,128)}), (f32[2,8192,2]{1,2,0:T(2,128)}, f32[8192,2]{0,1:T(2,128)})) %all-reduce.3.cloned.1.call-update) | async-done | bytes 196624 | tf_op jit(solution)/shard_map/psum | solution.py:193
  603.5 4.0 multiply_reduce_fusion
  607.5 9.8 %psum.23 = f32[2,24]{1,0:T(2,128)S(1)} all-reduce(f32[2,24]{1,0:T(2,128)S(1)} %get-tuple-element.952), channel_id=1, replica_groups=mesh['ka'=4,'gy'=8] {'ka'}, use_global_device_ids=true, to_apply=%region_17.18 | all-reduce | flops 48 | bytes 384 | tf_op jit(solution)/shard_map/psum | solution.py:195
  (338 shorter events, 253.7 us)
Async XLA Ops:
  7.2 174.7 %all-gather.13.cloned.1.call-start = ((), (), s32[]{:S(2)}) async-start(), calls=%async_computation | async-start | bytes 1769472 | tf_op jit(solution)/shard_map/all_gather | solution.py:32
  12.3 9.3 %collective-permute-start = (f32[2,8192,2,1]{1,2,0,3:T(2,128)}, f32[2,8192,2,1]{1,2,0,3:T(2,128)}, u32[]{:S(2)}, u32[]{:S(2)}) collective-permute-start(f32[2,8192,2,1]{1,2,0,3:T(2,128)} %get-tuple-element.966), channel_id=1, source_target_pairs={{0,1},{1,2},{2,3},{3,4},{4,5},{5,6},{6,7},{8,9},{9,10},{10,11},{11... | collective-permute-start | bytes 393224 | tf_op jit(solution)/shard_map/ppermute | solution.py:22
  15.3 6.2 collective-permute-start.1
  28.5 4.5 copy-start.3
  28.5 4.5 copy-start.4
  28.5 4.5 copy-start.5
  28.5 4.5 copy-start.6
  28.6 4.5 copy-start.7
  96.2 0.7 copy-start
  96.2 0.7 copy-start.1
  96.9 85.0 %all-gather.15.cloned.1.call-start = ((), (), s32[]{:S(2)}) async-start(), calls=%async_computation.1 | async-start | bytes 1769472 | tf_op jit(solution)/shard_map/all_gather | solution.py:32
  97.7 266.3 %all-gather.17.cloned.1.call-start = ((), (), s32[]{:S(2)}) async-start(), calls=%async_computation.2 | async-start | bytes 1769472 | tf_op jit(solution)/shard_map/all_gather | solution.py:32
  336.0 0.7 copy-start.2
  336.7 265.8 %all-reduce.3.cloned.1.call-start = ((), (), s32[]{:S(2)}) async-start(), calls=%async_computation.3 | async-start | bytes 393216 | tf_op jit(solution)/shard_map/psum | solution.py:193
Sparse Core Ops, SparseCore 0:
  97.0 32.7 all-gather.12
  131.5 27.3 all-gather.14
  336.9 27.0 all-gather.16
  548.0 54.4 all-reduce.2
where the time goes:
time: 635 us; the launch traced here: 624 us
  other arithmetic  276 us (43%)
  local copies, waits for them, and re-layouts  151 us (24%)
  blocking collectives  110 us (17%)
  waiting for transfers between devices  66.6 us (10%)
  between operations  14.1 us (2%)
    dynamic_update_slice x48, local copies, waits for them, and re-layouts, eliminate(): return lax.scan(advance, (factor_in, offset_in), stacked)[1]  121 us
    all_gather x6, blocking collectives, carried_in(): everything = jax.tree.map(lambda part: lax.all_gather(part, axis), x)  100 us
    dynamic_update_slice x48, other arithmetic, eliminate(): return lax.scan(advance, (factor_in, offset_in), stacked)[1]  81.8 us
    div x72, other arithmetic, compose(): member / largest  62.4 us
    psum x1, waiting for transfers between devices, per_device(): lax.psum((jnp.sum(columns[:2], axis=-1), jnp.sum(columns[2], axis=-1)), '...  54.7 us
    select_n x32, other arithmetic, lap(): return jax.tree.map(lambda a, b: jnp.where(reached, a, b), new, before)  28.7 us
    sub x24, other arithmetic, fold_back(): row_offset - line_multiplier * shift_now  28.5 us
    sub x24, other arithmetic, retreat(): result = row_offset - line_multiplier * running  25.3 us
  transfers between devices with their start and end apart: 6, of which 2 were waited for; matrix products, arithmetic and copies ran while one was open for 1% of the time, Pallas kernels for 0%

commit v1 on v0

v1 whole, which is shorter than its diff:
```python
import functools

import jax
import jax.numpy as jnp
import numpy as np
from jax import lax
from jax.experimental import pallas as pl
from jax.experimental.pallas import tpu as pltpu
from jax.sharding import PartitionSpec as P

MODES_Z = 512
LANES = 128
MESH = pl.DeviceIdType.MESH

viscous_rate = 400.0
wave_x = 1.0
wave_z = 2.0


def weight_table(total_rows):
    nch = 2 * total_rows
    rows = np.arange(total_rows + 1)
    order = 2 * rows[None, :] + np.arange(2)[:, None]
    top = np.broadcast_to((rows == 0)[None, :], order.shape)
    degree = np.where(top, 4, order).astype(np.float64)
    lower = np.where(order == 2, 2.0, 1.0) / (4.0 * degree * (degree - 1.0))
    middle = np.where(order <= nch - 3, 1.0, 0.0) / (2.0 * (degree * degree - 1.0))
    upper = np.where(order + 2 <= nch - 3, 1.0, 0.0) / (4.0 * degree * (degree + 1.0))
    lower, middle, upper = (np.where(top, 0.0, w) for w in (lower, middle, upper))
    cross = upper[:, :-1] * lower[:, 1:]
    return np.stack([lower[:, :-1], middle[:, :-1], upper[:, :-1], cross]).astype(np.float32).reshape(-1)


def shift_of(first_pair, rows):
    shape = (rows, LANES)
    pair = first_pair + lax.broadcasted_iota(jnp.int32, shape, 0) * LANES + lax.broadcasted_iota(jnp.int32, shape, 1)
    col_x = lax.shift_right_logical(pair, MODES_Z.bit_length() - 1)
    col_z = lax.bitwise_and(pair, MODES_Z - 1)
    signed = jnp.where(col_z < MODES_Z // 2, col_z, col_z - MODES_Z)
    kx = wave_x * col_x.astype(jnp.float32)
    kz = wave_z * signed.astype(jnp.float32)
    return kx * kx + kz * kz + viscous_rate


def row_factors(w_ref, total, q, row, local, last, lam, lam2, s_next):
    at = lambda k: w_ref[(2 * k + q) * total + row]
    pivot = 1.0 + lam * at(1)
    if local < last:
        pivot = pivot - lam2 * at(3) * s_next
    s = 1.0 / pivot
    low = lam * at(0)
    if local == 0:
        low = low + jnp.where(row == 0, 1.0, 0.0)
    return s, low * s, lam * at(2)


def reduce_kernel(n, per, rows, tile, group, w_ref, f_hbm, out_ref,
                  f_buf, y_send, y_recv, coef, elim, b_send, b_recv,
                  load_sem, ysend_sem, yrecv_sem, bsend_sem, brecv_sem):
    total = n * rows
    last = rows - 1
    me = lax.axis_index("gy")
    ka = lax.axis_index("ka")
    pairs = n * per * LANES
    span = group * per * tile
    groups = n // group
    first = lax.rem(me // group + 1, groups)

    def load(i):
        g = lax.rem(first + i, groups)
        where = pl.ds(pl.multiple_of(g * span, span), span)
        return pltpu.make_async_copy(f_hbm.at[:, :, :, where, :], f_buf.at[:, :, :, where, :], load_sem.at[i])

    for i in range(groups):
        load(i).start()

    barrier = pltpu.get_barrier_semaphore()

    def greet(k, _):
        pl.semaphore_signal(barrier, inc=1, device_id={"gy": lax.rem(me + k, n)}, device_id_type=MESH)
        return 0

    lax.fori_loop(1, n, greet, 0)

    def y_copy(to, frm):
        return pltpu.make_async_remote_copy(
            src_ref=y_send.at[to], dst_ref=y_recv.at[frm], send_sem=ysend_sem.at[to],
            recv_sem=yrecv_sem.at[frm], device_id={"gy": to}, device_id_type=MESH)

    def b_copy(to, frm):
        return pltpu.make_async_remote_copy(
            src_ref=b_send.at[to], dst_ref=b_recv.at[frm], send_sem=bsend_sem.at[to],
            recv_sem=brecv_sem.at[frm], device_id={"gy": to}, device_id_type=MESH)

    def local_group(i, _):
        g = lax.rem(first + i, groups)
        load(i).wait()
        lam = shift_of(ka * pairs + g * (group * per * LANES), group * per)
        lam2 = lam * lam
        kappa = viscous_rate / lam
        for q in range(2):
            s = None
            e = [None, None]
            yl = [None, None]
            sums = [None, None]
            for j in range(last, -1, -1):
                row = me * rows + j
                s, ls, up = row_factors(w_ref, total, q, row, j, last, lam, lam2, s)
                for p in range(2):
                    f = f_buf[p, q, j // tile, pl.ds(g * span + j % tile, group * per, stride=tile), :]
                    src = kappa * f
                    if j == last:
                        e[p] = s * src
                        yl[p] = e[p]
                        sums[p] = e[p] - src
                    else:
                        e[p] = s * (src + up * e[p])
                        yl[p] = yl[p] + carry * e[p]
                        sums[p] = sums[p] + (theta * e[p] - src)
                if j == last:
                    carry = ls
                    theta = 1.0 + ls
                else:
                    carry = carry * ls
                    theta = 1.0 + ls * theta
            for p in range(2):
                for k, value in enumerate((e[p], yl[p], sums[p])):
                    for m in range(group):
                        y_send[g * group + m, k, p, q] = value[m * per:(m + 1) * per]

        @pl.when(i == 0)
        def _():
            pl.semaphore_wait(barrier, n - 1)

        for m in range(group):
            to = g * group + m

            @pl.when(to != me)
            def _():
                y_copy(to, me).start()
        return 0

    lax.fori_loop(0, groups, local_group, 0)
    y_recv[me] = y_send[me]

    lam = shift_of(ka * pairs + me * (per * LANES), per)
    lam2 = lam * lam
    unroll = 4 if n % 4 == 0 else 1

    def responses(i, _):
        for d in range(unroll):
            block = i * unroll + d
            for q in range(2):
                s = None
                for j in range(last, -1, -1):
                    row = block * rows + j
                    s, ls, up = row_factors(w_ref, total, q, row, j, last, lam, lam2, s)
                    if j == last:
                        e = s * up
                        yl = e
                        sums = e
                        carry = ls
                        tau = ls
                    else:
                        e = s * (up * e)
                        yl = yl + carry * e
                        sums = sums + (1.0 + tau) * e
                        carry = carry * ls
                        tau = ls * (1.0 + tau)
                for k, value in enumerate((ls, e, carry, yl, tau, sums)):
                    coef[block, k, q] = value
        return 0

    lax.fori_loop(0, n // unroll, responses, 0)

    def y_arrived(k, _):
        y_copy(me, lax.rem(me + k, n)).wait_recv()
        return 0

    lax.fori_loop(1, n, y_arrived, 0)

    zero = jnp.zeros((2, per, LANES), jnp.float32)
    for k in range(3):
        elim[n, k] = zero

    def up_sweep(k, state):
        g = n - 1 - k
        f0, f1, phi, s0, s1, psi = state
        a, b, c, d, alpha, beta = (coef[g, m] for m in range(6))
        inv = 1.0 / (1.0 - d * phi)
        lamb = c * inv
        ls = [(y_recv[g, 1, p] + d * fp) * inv for p, fp in ((0, f0), (1, f1))]
        right = [fp + phi * l for fp, l in ((f0, ls[0]), (f1, ls[1]))]
        new_f = [y_recv[g, 0, p] + b * right[p] for p in range(2)]
        new_s = [y_recv[g, 2, p] + beta * right[p] + sp + psi * ls[p] for p, sp in ((0, s0), (1, s1))]
        new_phi = a + b * (phi * lamb)
        new_psi = alpha + beta * (phi * lamb) + psi * lamb
        elim[g, 0] = new_f[0]
        elim[g, 1] = new_f[1]
        elim[g, 2] = new_phi
        elim[g, 3] = ls[0]
        elim[g, 4] = ls[1]
        elim[g, 5] = lamb
        return new_f[0], new_f[1], new_phi, new_s[0], new_s[1], new_psi

    state = lax.fori_loop(0, n, up_sweep, (zero,) * 6)
    wall = 1.0 / state[5]

    def down_sweep(g, left):
        b_send[g, 0, 0] = left[0]
        b_send[g, 0, 1] = left[1]
        new = [elim[g, 3 + p] + elim[g, 5] * left[p] for p in range(2)]
        for p in range(2):
            b_send[g, 1, p] = elim[g + 1, p] + elim[g + 1, 2] * new[p]

        @pl.when(g != me)
        def _():
            b_copy(g, me).start()

        return new[0], new[1]

    lax.fori_loop(0, n, down_sweep, (-state[3] * wall, -state[4] * wall))
    b_recv[me] = b_send[me]
    out_ref[me] = b_recv[me]

    def b_arrived(k, _):
        frm = lax.rem(me + k, n)
        b_copy(me, frm).wait_recv()
        out_ref[frm] = b_recv[frm]
        return 0

    lax.fori_loop(1, n, b_arrived, 0)

    def sent(k, _):
        to = lax.rem(me + k, n)
        y_copy(to, me).wait_send()
        b_copy(to, me).wait_send()
        return 0

    lax.fori_loop(1, n, sent, 0)


def close_kernel(n, per, rows, tile, group, w_ref, f_ref, b_ref, x_ref, sq_ref, e_buf, ls_buf):
    total = n * rows
    last = rows - 1
    me = lax.axis_index("gy")
    ka = lax.axis_index("ka")
    i = pl.program_id(0)
    count = group * per

    @pl.when(i == 0)
    def _():
        sq_ref[...] = jnp.zeros_like(sq_ref)

    lam = shift_of(ka * (n * per * LANES) + i * (count * LANES), count)
    lam2 = lam * lam
    kappa = viscous_rate / lam
    joined = lambda k, p, q: jnp.concatenate([b_ref[m, k, p, q] for m in range(group)], axis=0)
    for q in range(2):
        s = None
        e = [joined(1, p, q) for p in range(2)]
        for j in range(last, -1, -1):
            s, ls, up = row_factors(w_ref, total, q, me * rows + j, j, last, lam, lam2, s)
            ls_buf[q, j] = ls
            for p in range(2):
                f = f_ref[p, q, j // tile, pl.ds(j % tile, count, stride=tile), :]
                e[p] = s * (kappa * f + up * e[p])
                e_buf[q, p, j] = e[p]
        z = [joined(0, p, q) for p in range(2)]
        for j in range(rows):
            square = None
            for p in range(2):
                where = (p, q, j // tile, pl.ds(j % tile, count, stride=tile), slice(None))
                z[p] = e_buf[q, p, j] + ls_buf[q, j] * z[p]
                x = z[p] - kappa * f_ref[where]
                x_ref[where] = x
                square = x * x if p == 0 else square + x * x
            sq_ref[q, j] += sum(square[m * per:(m + 1) * per] for m in range(group))


def spectrum_kernel(nk, rows, scale, sq_ref, out_ref, mine, held, send_sem, recv_sem):
    me = lax.axis_index("ka")
    barrier = pltpu.get_barrier_semaphore()
    for k in range(1, nk):
        pl.semaphore_signal(barrier, inc=1, device_id={"ka": lax.rem(me + k, nk)}, device_id_type=MESH)
    mine[...] = jnp.sum(sq_ref[...], axis=2)
    pl.semaphore_wait(barrier, nk - 1)

    def copy(k):
        return pltpu.make_async_remote_copy(
            src_ref=mine, dst_ref=held.at[k - 1], send_sem=send_sem.at[k - 1], recv_sem=recv_sem.at[k - 1],
            device_id={"ka": lax.rem(me + k, nk)}, device_id_type=MESH)

    for k in range(1, nk):
        copy(k).start()
    added = mine[...]
    for k in range(1, nk):
        copy(k).wait_recv()
        added = added + held[k - 1]
    ones = jnp.ones((8, LANES), jnp.float32)
    for q in range(2):
        sums = lax.dot_general(ones, added[q], (((1,), (1,)), ((), ())), precision=lax.Precision.HIGHEST,
                               preferred_element_type=jnp.float32)
        out_ref[q:q + 1, :] = sums[0:1] * scale
    for k in range(1, nk):
        copy(k).wait_send()


def per_device(n, nk, driving_coefficients):
    _, pairs, _, rows = driving_coefficients.shape
    per = pairs // (LANES * n)
    tile = 8 if rows % 8 == 0 else 1
    cols = pairs // LANES
    group = next((g for g in range(2, n) if n % g == 0 and g * per * tile % 8 == 0), n)
    span = group * per * tile
    f = jnp.transpose(driving_coefficients, (0, 2, 3, 1)).reshape(2, 2, rows // tile, tile, cols, LANES)
    f = jnp.swapaxes(f, 3, 4).reshape(2, 2, rows // tile, cols * tile, LANES)
    table = jnp.asarray(weight_table(n * rows))
    smem = pl.BlockSpec(memory_space=pltpu.SMEM)
    vmem = pl.BlockSpec(memory_space=pltpu.VMEM)
    f32 = jnp.float32
    edges = pl.pallas_call(
        functools.partial(reduce_kernel, n, per, rows, tile, group),
        out_shape=jax.ShapeDtypeStruct((n, 2, 2, 2, per, LANES), f32),
        in_specs=[smem, pl.BlockSpec(memory_space=pl.ANY)],
        out_specs=vmem,
        scratch_shapes=[
            pltpu.VMEM(f.shape, f32),
            pltpu.VMEM((n, 3, 2, 2, per, LANES), f32),
            pltpu.VMEM((n, 3, 2, 2, per, LANES), f32),
            pltpu.VMEM((n, 6, 2, per, LANES), f32),
            pltpu.VMEM((n + 1, 6, 2, per, LANES), f32),
            pltpu.VMEM((n, 2, 2, 2, per, LANES), f32),
            pltpu.VMEM((n, 2, 2, 2, per, LANES), f32),
            pltpu.SemaphoreType.DMA((n // group,)),
            pltpu.SemaphoreType.DMA((n,)),
            pltpu.SemaphoreType.DMA((n,)),
            pltpu.SemaphoreType.DMA((n,)),
            pltpu.SemaphoreType.DMA((n,)),
        ],
        compiler_params=pltpu.CompilerParams(collective_id=0, has_side_effects=True),
        name="reduce_blocks",
    )(table, f)
    block = (2, 2, rows // tile, span, LANES)
    x, squares = pl.pallas_call(
        functools.partial(close_kernel, n, per, rows, tile, group),
        grid=(n // group,),
        out_shape=(jax.ShapeDtypeStruct(f.shape, f32), jax.ShapeDtypeStruct((2, rows, per, LANES), f32)),
        in_specs=[smem, pl.BlockSpec(block, lambda i: (0, 0, 0, i, 0)),
                  pl.BlockSpec((group, 2, 2, 2, per, LANES), lambda i: (i, 0, 0, 0, 0, 0))],
        out_specs=(pl.BlockSpec(block, lambda i: (0, 0, 0, i, 0)),
                   pl.BlockSpec((2, rows, per, LANES), lambda i: (0, 0, 0, 0))),
        scratch_shapes=[pltpu.VMEM((2, 2, rows, group * per, LANES), f32), pltpu.VMEM((2, rows, group * per, LANES), f32)],
        name="close_blocks",
    )(table, f, edges)
    spectrum = pl.pallas_call(
        functools.partial(spectrum_kernel, nk, rows, 1.0 / (2.0 * pairs * nk)),
        out_shape=jax.ShapeDtypeStruct((2, rows), f32),
        in_specs=[vmem],
        out_specs=vmem,
        scratch_shapes=[
            pltpu.VMEM((2, rows, LANES), f32),
            pltpu.VMEM((nk - 1, 2, rows, LANES), f32),
            pltpu.SemaphoreType.DMA((nk - 1,)),
            pltpu.SemaphoreType.DMA((nk - 1,)),
        ],
        compiler_params=pltpu.CompilerParams(collective_id=1, has_side_effects=True),
        name="spectrum_over_ka",
    )(squares)
    x = jnp.swapaxes(x.reshape(2, 2, rows // tile, cols, tile, LANES), 3, 4).reshape(2, 2, rows, pairs)
    return jnp.transpose(x, (0, 3, 1, 2)), spectrum


def solution(mesh):
    n, nk = mesh.shape["gy"], mesh.shape["ka"]
    return jax.shard_map(
        functools.partial(per_device, n, nk), mesh=mesh,
        in_specs=(P(None, "ka", None, "gy"),),
        out_specs=(P(None, "ka", None, "gy"), P(None, "gy")), check_vma=False,
    )
```

time: 635 us -> 36.4 us (0.06); the launches traced: 624 us -> 36.1 us
  other arithmetic: 276 us -> 0 us
  local copies, waits for them, and re-layouts: 151 us -> 1.22 us
  blocking collectives: 110 us -> 0 us
  waiting for transfers between devices: 66.6 us -> 0 us
  Pallas kernels: 0 us -> 34.3 us
  between operations: 14.1 us -> 0.65 us
    dynamic_update_slice x48 -> x0, local copies, waits for them, and re-layouts: 121 us -> none  [eliminate(): return lax.scan(advance, (factor_in, offset_in), stacked)[1]]
    all_gather x6 -> x0, blocking collectives: 100 us -> none  [carried_in(): everything = jax.tree.map(lambda part: lax.all_gather(part, axis), x)]
    dynamic_update_slice x48 -> x0, other arithmetic: 81.8 us -> none  [eliminate(): return lax.scan(advance, (factor_in, offset_in), stacked)[1]]
    div x76 -> x0, other arithmetic: 64.1 us -> none  [the longest x72 62.4 us: compose(): member / largest]
    psum x1 -> x0, waiting for transfers between devices: 54.7 us -> none  [per_device(): lax.psum((jnp.sum(columns[:2], axis=-1), jnp.sum(columns[2], axis=-1)), '...]
    sub x48 -> x0, other arithmetic: 53.8 us -> none  [the longest x24 28.5 us: fold_back(): row_offset - line_multiplier * shift_now]
    pallas_call x0 -> x3, Pallas kernels: none -> 34.3 us  [the longest x1 21.7 us: per_device(): pl.pallas_call(functools.partial(reduce_kernel, n, per, rows, tile, group...]
    select_n x36 -> x0, other arithmetic: 33.5 us -> none  [the longest x32 28.7 us: lap(): return jax.tree.map(lambda a, b: jnp.where(reached, a, b), new, before)]
  transfers between devices with their start and end apart: 6 -> 0, of which waited for: 2 -> 0; matrix products, arithmetic and copies ran while one was open for 1% -> 0% of each run, Pallas kernels for 0% -> 0%
where the time goes in v1:
time: 36.4 us; the launch traced here: 36.1 us
  Pallas kernels  34.3 us (94%)
  local copies, waits for them, and re-layouts  1.22 us (3%)
  between operations  0.65 us (2%)
    pallas_call x1, Pallas kernels, per_device(): pl.pallas_call(functools.partial(reduce_kernel, n, per, rows, tile, group...  21.7 us
    pallas_call x1, Pallas kernels, per_device(): pl.pallas_call(functools.partial(spectrum_kernel, nk, rows, 1.0 / (2.0 *...  6.88 us
    pallas_call x1, Pallas kernels, per_device(): pl.pallas_call(functools.partial(close_kernel, n, per, rows, tile, group)...  5.66 us
    unnamed x1, local copies, waits for them, and re-layouts  1.22 us

profile of v1, /device:TPU:0, one launch (start us, length us, event | category | flops | bytes accessed | tf_op | source)
XLA Modules:
  0.0 36.1 jit_solution(12317104118613390551)
XLA Ops:
  0.6 21.7 %reduce_blocks.1.b_ref = f32[8,2,2,2,8,128]{5,4,3,2,1,0:T(8,128)} custom-call(f32[1536]{0:T(1024)} %constant.2.clone.w_ref, f32[2,2,3,512,128]{4,3,2,1,0:T(8,128)} %bitcast.14), custom_call_target="tpu_custom_call" | custom-call | tf_op jit(solution)/shard_map/reduce_blocks/pallas_call | solution.py:322
  22.4 5.7 %close_blocks.1 = (f32[2,2,3,512,128]{4,3,2,1,0:T(8,128)}, f32[2,24,8,128]{3,2,1,0:T(8,128)}) custom-call(f32[1536]{0:T(1024)} %constant.2.clone.w_ref, f32[2,2,3,512,128]{4,3,2,1,0:T(8,128)} %bitcast.15, f32[8,2,2,2,8,128]{5,4,3,2,1,0:T(8,128)} %reduce_blocks.1.b_ref), custom_call_target="tpu_custom_call" | custom-call | tf_op jit(solution)/shard_map/close_blocks/pallas_call | solution.py:345
  28.0 6.9 %spectrum_over_ka.1 = f32[2,24]{1,0:T(2,128)} custom-call(f32[2,24,8,128]{3,2,1,0:T(8,128)} %get-tuple-element.5.sq_ref), custom_call_target="tpu_custom_call" | custom-call | tf_op jit(solution)/shard_map/spectrum_over_ka/pallas_call | solution.py:356
  34.9 1.2 %copy.5 = f32[2,24]{1,0:T(2,128)} copy(f32[2,24]{1,0:T(2,128)} %spectrum_over_ka.1) | data formatting | bytes 384

commit v2 on v1

--- a/solution.py
+++ b/solution.py
@@ -54,23 +54,31 @@
     return s, low * s, lam * at(2)
 
 
-def reduce_kernel(n, per, rows, tile, group, w_ref, f_hbm, out_ref,
-                  f_buf, y_send, y_recv, coef, elim, b_send, b_recv,
-                  load_sem, ysend_sem, yrecv_sem, bsend_sem, brecv_sem):
+def channel_kernel(n, nk, per, rows, tile, group, scale, w_ref, f_hbm, x_hbm, spec_ref,
+                   f_buf, x_buf, e_buf, ls_buf, r_buf, sq_buf, y_send, y_recv, coef, elim, b_send, b_recv, mine, held,
+                   load_sem, store_sem, ysend_sem, yrecv_sem, bsend_sem, brecv_sem, ssend_sem, srecv_sem):
     total = n * rows
     last = rows - 1
     me = lax.axis_index("gy")
     ka = lax.axis_index("ka")
     pairs = n * per * LANES
-    span = group * per * tile
+    count = group * per
+    span = count * tile
     groups = n // group
-    first = lax.rem(me // group + 1, groups)
+
+    def nearest(k, here, size):
+        return lax.bitwise_xor(here, k) if size & (size - 1) == 0 else lax.rem(here + k, size)
 
     def load(i):
-        g = lax.rem(first + i, groups)
+        g = nearest(groups - 1 - i, me // group, groups)
         where = pl.ds(pl.multiple_of(g * span, span), span)
         return pltpu.make_async_copy(f_hbm.at[:, :, :, where, :], f_buf.at[:, :, :, where, :], load_sem.at[i])
 
+    def store(i):
+        g = nearest(i, me // group, groups)
+        where = pl.ds(pl.multiple_of(g * span, span), span)
+        return pltpu.make_async_copy(x_buf.at[:, :, :, where, :], x_hbm.at[:, :, :, where, :], store_sem.at[i])
+
     for i in range(groups):
         load(i).start()
 
@@ -81,6 +89,8 @@
         return 0
 
     lax.fori_loop(1, n, greet, 0)
+    for k in range(1, nk):
+        pl.semaphore_signal(barrier, inc=1, device_id={"ka": lax.rem(ka + k, nk)}, device_id_type=MESH)
 
     def y_copy(to, frm):
         return pltpu.make_async_remote_copy(
@@ -93,9 +103,10 @@
             recv_sem=brecv_sem.at[frm], device_id={"gy": to}, device_id_type=MESH)
 
     def local_group(i, _):
-        g = lax.rem(first + i, groups)
+        g = nearest(groups - 1 - i, me // group, groups)
         load(i).wait()
-        lam = shift_of(ka * pairs + g * (group * per * LANES), group * per)
+        part = pl.ds(pl.multiple_of(g * count, count), count)
+        lam = shift_of(ka * pairs + g * (count * LANES), count)
         lam2 = lam * lam
         kappa = viscous_rate / lam
         for q in range(2):
@@ -106,8 +117,11 @@
             for j in range(last, -1, -1):
                 row = me * rows + j
                 s, ls, up = row_factors(w_ref, total, q, row, j, last, lam, lam2, s)
+                right = s * up if j == last else (s * up) * right
+                ls_buf[q, j, part] = ls
+                r_buf[q, j, part] = right
                 for p in range(2):
-                    f = f_buf[p, q, j // tile, pl.ds(g * span + j % tile, group * per, stride=tile), :]
+                    f = f_buf[p, q, j // tile, pl.ds(g * span + j % tile, count, stride=tile), :]
                     src = kappa * f
                     if j == last:
                         e[p] = s * src
@@ -117,6 +131,7 @@
                         e[p] = s * (src + up * e[p])
                         yl[p] = yl[p] + carry * e[p]
                         sums[p] = sums[p] + (theta * e[p] - src)
+                    e_buf[p, q, j, part] = e[p]
                 if j == last:
                     carry = ls
                     theta = 1.0 + ls
@@ -130,7 +145,7 @@
 
         @pl.when(i == 0)
         def _():
-            pl.semaphore_wait(barrier, n - 1)
+            pl.semaphore_wait(barrier, n + nk - 2)
 
         for m in range(group):
             to = g * group + m
@@ -221,15 +236,49 @@
 
     lax.fori_loop(0, n, down_sweep, (-state[3] * wall, -state[4] * wall))
     b_recv[me] = b_send[me]
-    out_ref[me] = b_recv[me]
-
-    def b_arrived(k, _):
-        frm = lax.rem(me + k, n)
-        b_copy(me, frm).wait_recv()
-        out_ref[frm] = b_recv[frm]
-        return 0
-
-    lax.fori_loop(1, n, b_arrived, 0)
+    sq_buf[...] = jnp.zeros_like(sq_buf)
+
+    def close_group(i, _):
+        g = nearest(i, me // group, groups)
+        for m in range(group):
+            frm = g * group + m
+
+            @pl.when(frm != me)
+            def _():
+                b_copy(me, frm).wait_recv()
+
+        part = pl.ds(pl.multiple_of(g * count, count), count)
+        lam = shift_of(ka * pairs + g * (count * LANES), count)
+        kappa = viscous_rate / lam
+        joined = lambda k, p, q: jnp.concatenate([b_recv[g * group + m, k, p, q] for m in range(group)], axis=0)
+        for q in range(2):
+            z = [joined(0, p, q) for p in range(2)]
+            after = [joined(1, p, q) for p in range(2)]
+            for j in range(rows):
+                ls = ls_buf[q, j, part]
+                right = r_buf[q, j, part]
+                square = None
+                for p in range(2):
+                    where = (p, q, j // tile, pl.ds(g * span + j % tile, count, stride=tile), slice(None))
+                    z[p] = (e_buf[p, q, j, part] + right * after[p]) + ls * z[p]
+                    x = z[p] - kappa * f_buf[where]
+                    x_buf[where] = x
+                    square = x * x if p == 0 else square + x * x
+                sq_buf[q, j] += sum(square[m * per:(m + 1) * per] for m in range(group))
+        store(i).start()
+        return 0
+
+    lax.fori_loop(0, groups, close_group, 0)
+
+    mine[...] = jnp.sum(sq_buf[...], axis=2)
+
+    def s_copy(k):
+        return pltpu.make_async_remote_copy(
+            src_ref=mine, dst_ref=held.at[k - 1], send_sem=ssend_sem.at[k - 1], recv_sem=srecv_sem.at[k - 1],
+            device_id={"ka": lax.rem(ka + k, nk)}, device_id_type=MESH)
+
+    for k in range(1, nk):
+        s_copy(k).start()
 
     def sent(k, _):
         to = lax.rem(me + k, n)
@@ -238,72 +287,19 @@
         return 0
 
     lax.fori_loop(1, n, sent, 0)
-
-
-def close_kernel(n, per, rows, tile, group, w_ref, f_ref, b_ref, x_ref, sq_ref, e_buf, ls_buf):
-    total = n * rows
-    last = rows - 1
-    me = lax.axis_index("gy")
-    ka = lax.axis_index("ka")
-    i = pl.program_id(0)
-    count = group * per
-
-    @pl.when(i == 0)
-    def _():
-        sq_ref[...] = jnp.zeros_like(sq_ref)
-
-    lam = shift_of(ka * (n * per * LANES) + i * (count * LANES), count)
-    lam2 = lam * lam
-    kappa = viscous_rate / lam
-    joined = lambda k, p, q: jnp.concatenate([b_ref[m, k, p, q] for m in range(group)], axis=0)
-    for q in range(2):
-        s = None
-        e = [joined(1, p, q) for p in range(2)]
-        for j in range(last, -1, -1):
-            s, ls, up = row_factors(w_ref, total, q, me * rows + j, j, last, lam, lam2, s)
-            ls_buf[q, j] = ls
-            for p in range(2):
-                f = f_ref[p, q, j // tile, pl.ds(j % tile, count, stride=tile), :]
-                e[p] = s * (kappa * f + up * e[p])
-                e_buf[q, p, j] = e[p]
-        z = [joined(0, p, q) for p in range(2)]
-        for j in range(rows):
-            square = None
-            for p in range(2):
-                where = (p, q, j // tile, pl.ds(j % tile, count, stride=tile), slice(None))
-                z[p] = e_buf[q, p, j] + ls_buf[q, j] * z[p]
-                x = z[p] - kappa * f_ref[where]
-                x_ref[where] = x
-                square = x * x if p == 0 else square + x * x
-            sq_ref[q, j] += sum(square[m * per:(m + 1) * per] for m in range(group))
-
-
-def spectrum_kernel(nk, rows, scale, sq_ref, out_ref, mine, held, send_sem, recv_sem):
-    me = lax.axis_index("ka")
-    barrier = pltpu.get_barrier_semaphore()
-    for k in range(1, nk):
-        pl.semaphore_signal(barrier, inc=1, device_id={"ka": lax.rem(me + k, nk)}, device_id_type=MESH)
-    mine[...] = jnp.sum(sq_ref[...], axis=2)
-    pl.semaphore_wait(barrier, nk - 1)
-
-    def copy(k):
-        return pltpu.make_async_remote_copy(
-            src_ref=mine, dst_ref=held.at[k - 1], send_sem=send_sem.at[k - 1], recv_sem=recv_sem.at[k - 1],
-            device_id={"ka": lax.rem(me + k, nk)}, device_id_type=MESH)
-
-    for k in range(1, nk):
-        copy(k).start()
     added = mine[...]
     for k in range(1, nk):
-        copy(k).wait_recv()
+        s_copy(k).wait_recv()
         added = added + held[k - 1]
     ones = jnp.ones((8, LANES), jnp.float32)
     for q in range(2):
         sums = lax.dot_general(ones, added[q], (((1,), (1,)), ((), ())), precision=lax.Precision.HIGHEST,
                                preferred_element_type=jnp.float32)
-        out_ref[q:q + 1, :] = sums[0:1] * scale
+        spec_ref[q:q + 1, :] = sums[0:1] * scale
     for k in range(1, nk):
-        copy(k).wait_send()
+        s_copy(k).wait_send()
+    for i in range(groups):
+        store(i).wait()
 
 
 def per_device(n, nk, driving_coefficients):
@@ -319,54 +315,38 @@
     smem = pl.BlockSpec(memory_space=pltpu.SMEM)
     vmem = pl.BlockSpec(memory_space=pltpu.VMEM)
     f32 = jnp.float32
-    edges = pl.pallas_call(
-        functools.partial(reduce_kernel, n, per, rows, tile, group),
-        out_shape=jax.ShapeDtypeStruct((n, 2, 2, 2, per, LANES), f32),
+    x, spectrum = pl.pallas_call(
+        functools.partial(channel_kernel, n, nk, per, rows, tile, group, 1.0 / (2.0 * pairs * nk)),
+        out_shape=(jax.ShapeDtypeStruct(f.shape, f32), jax.ShapeDtypeStruct((2, rows), f32)),
         in_specs=[smem, pl.BlockSpec(memory_space=pl.ANY)],
-        out_specs=vmem,
+        out_specs=(pl.BlockSpec(memory_space=pl.ANY), vmem),
         scratch_shapes=[
             pltpu.VMEM(f.shape, f32),
+            pltpu.VMEM(f.shape, f32),
+            pltpu.VMEM((2, 2, rows, cols, LANES), f32),
+            pltpu.VMEM((2, rows, cols, LANES), f32),
+            pltpu.VMEM((2, rows, cols, LANES), f32),
+            pltpu.VMEM((2, rows, per, LANES), f32),
             pltpu.VMEM((n, 3, 2, 2, per, LANES), f32),
             pltpu.VMEM((n, 3, 2, 2, per, LANES), f32),
             pltpu.VMEM((n, 6, 2, per, LANES), f32),
             pltpu.VMEM((n + 1, 6, 2, per, LANES), f32),
             pltpu.VMEM((n, 2, 2, 2, per, LANES), f32),
             pltpu.VMEM((n, 2, 2, 2, per, LANES), f32),
+            pltpu.VMEM((2, rows, LANES), f32),
+            pltpu.VMEM((nk - 1, 2, rows, LANES), f32),
+            pltpu.SemaphoreType.DMA((n // group,)),
             pltpu.SemaphoreType.DMA((n // group,)),
             pltpu.SemaphoreType.DMA((n,)),
             pltpu.SemaphoreType.DMA((n,)),
             pltpu.SemaphoreType.DMA((n,)),
             pltpu.SemaphoreType.DMA((n,)),
-        ],
-        compiler_params=pltpu.CompilerParams(collective_id=0, has_side_effects=True),
-        name="reduce_blocks",
-    )(table, f)
-    block = (2, 2, rows // tile, span, LANES)
-    x, squares = pl.pallas_call(
-        functools.partial(close_kernel, n, per, rows, tile, group),
-        grid=(n // group,),
-        out_shape=(jax.ShapeDtypeStruct(f.shape, f32), jax.ShapeDtypeStruct((2, rows, per, LANES), f32)),
-        in_specs=[smem, pl.BlockSpec(block, lambda i: (0, 0, 0, i, 0)),
-                  pl.BlockSpec((group, 2, 2, 2, per, LANES), lambda i: (i, 0, 0, 0, 0, 0))],
-        out_specs=(pl.BlockSpec(block, lambda i: (0, 0, 0, i, 0)),
-                   pl.BlockSpec((2, rows, per, LANES), lambda i: (0, 0, 0, 0))),
-        scratch_shapes=[pltpu.VMEM((2, 2, rows, group * per, LANES), f32), pltpu.VMEM((2, rows, group * per, LANES), f32)],
-        name="close_blocks",
-    )(table, f, edges)
-    spectrum = pl.pallas_call(
-        functools.partial(spectrum_kernel, nk, rows, 1.0 / (2.0 * pairs * nk)),
-        out_shape=jax.ShapeDtypeStruct((2, rows), f32),
-        in_specs=[vmem],
-        out_specs=vmem,
-        scratch_shapes=[
-            pltpu.VMEM((2, rows, LANES), f32),
-            pltpu.VMEM((nk - 1, 2, rows, LANES), f32),
             pltpu.SemaphoreType.DMA((nk - 1,)),
             pltpu.SemaphoreType.DMA((nk - 1,)),
         ],
-        compiler_params=pltpu.CompilerParams(collective_id=1, has_side_effects=True),
-        name="spectrum_over_ka",
-    )(squares)
+        compiler_params=pltpu.CompilerParams(collective_id=0, has_side_effects=True),
+        name="channel_substep",
+    )(table, f)
     x = jnp.swapaxes(x.reshape(2, 2, rows // tile, cols, tile, LANES), 3, 4).reshape(2, 2, rows, pairs)
     return jnp.transpose(x, (0, 3, 1, 2)), spectrum
 

time: 36.4 us -> 31.3 us (0.86)
  Pallas kernels: 34.3 us -> 26.1 us
  local copies, waits for them, and re-layouts: 1.22 us -> 4.32 us
    pallas_call x3 -> x1, Pallas kernels: 34.3 us -> 26.1 us  [per_device(): pl.pallas_call(functools.partial(channel_kernel, n, nk, per, rows, tile,...]
    unnamed x1 -> x4, local copies, waits for them, and re-layouts: 1.22 us -> 4.32 us
where the time goes in v2:
time: 31.3 us; the launch traced here: 31.1 us
  Pallas kernels  26.1 us (83%)
  local copies, waits for them, and re-layouts  4.32 us (14%)
  between operations  0.65 us (2%)
    pallas_call x1, Pallas kernels, per_device(): pl.pallas_call(functools.partial(channel_kernel, n, nk, per, rows, tile,...  26.1 us
    unnamed x4, local copies, waits for them, and re-layouts  4.32 us

profile of v2, /device:TPU:0, one launch (start us, length us, event | category | flops | bytes accessed | tf_op | source)
XLA Modules:
  0.0 31.1 jit_solution(12586862697415556592)
XLA Ops:
  0.6 26.1 %channel_substep.1 = (f32[2,2,3,512,128]{4,3,2,1,0:T(8,128)}, f32[2,24]{1,0:T(2,128)}) custom-call(f32[1536]{0:T(1024)} %constant.2.clone.w_ref, f32[2,2,3,512,128]{4,3,2,1,0:T(8,128)} %bitcast.14), custom_call_target="tpu_custom_call" | custom-call | tf_op jit(solution)/shard_map/channel_substep/pallas_call | solution.py:318
  26.8 0.0 copy-start
  26.8 3.8 %copy.6 = f32[2,8192,2,24]{1,3,2,0:T(8,128)} copy(f32[2,8192,2,24]{1,3,2,0:T(8,128)} %bitcast.15) | data formatting | bytes 6291456
  30.5 0.0 copy-done
  30.5 0.6 %copy.7 = f32[2,24]{1,0:T(2,128)} copy(f32[2,24]{1,0:T(2,128)S(1)} %copy-done) | data formatting | bytes 384
Async XLA Ops:
  26.8 3.8 %copy-start = (f32[2,24]{1,0:T(2,128)S(1)}, f32[2,24]{1,0:T(2,128)}, u32[]{:S(2)}) copy-start(f32[2,24]{1,0:T(2,128)} %get-tuple-element.9) | copy-start | bytes 580

commit v3 on v2

--- a/solution.py
+++ b/solution.py
@@ -55,8 +55,9 @@
 
 
 def channel_kernel(n, nk, per, rows, tile, group, scale, w_ref, f_hbm, x_hbm, spec_ref,
-                   f_buf, x_buf, e_buf, ls_buf, r_buf, sq_buf, y_send, y_recv, coef, elim, b_send, b_recv, mine, held,
-                   load_sem, store_sem, ysend_sem, yrecv_sem, bsend_sem, brecv_sem, ssend_sem, srecv_sem):
+                   f_buf, x_buf, e_buf, ls_buf, r_buf, sq_buf, both, y_send, y_recv, coef, elim, b_send, edge, mine, held,
+                   load_sem, store_sem, dsend_sem, drecv_sem, ysend_sem, yrecv_sem, bsend_sem, erecv_sem, rsend_sem,
+                   ssend_sem, srecv_sem):
     total = n * rows
     last = rows - 1
     me = lax.axis_index("gy")
@@ -65,6 +66,9 @@
     count = group * per
     span = count * tile
     groups = n // group
+    chips = n // 2
+    chip, core = me // 2, lax.rem(me, 2)
+    sibling = 2 * chip + 1 - core
 
     def nearest(k, here, size):
         return lax.bitwise_xor(here, k) if size & (size - 1) == 0 else lax.rem(here + k, size)
@@ -92,17 +96,28 @@
     for k in range(1, nk):
         pl.semaphore_signal(barrier, inc=1, device_id={"ka": lax.rem(ka + k, nk)}, device_id_type=MESH)
 
+    def d_copy(which, g):
+        where = pl.ds(g * group, group)
+        return pltpu.make_async_remote_copy(
+            src_ref=both.at[which, where], dst_ref=both.at[which, where], send_sem=dsend_sem.at[g],
+            recv_sem=drecv_sem.at[g], device_id={"gy": sibling}, device_id_type=MESH)
+
     def y_copy(to, frm):
         return pltpu.make_async_remote_copy(
             src_ref=y_send.at[to], dst_ref=y_recv.at[frm], send_sem=ysend_sem.at[to],
-            recv_sem=yrecv_sem.at[frm], device_id={"gy": to}, device_id_type=MESH)
-
-    def b_copy(to, frm):
+            recv_sem=yrecv_sem.at[frm], device_id={"gy": 2 * to + core}, device_id_type=MESH)
+
+    def b_copy(to, owner):
         return pltpu.make_async_remote_copy(
-            src_ref=b_send.at[to], dst_ref=b_recv.at[frm], send_sem=bsend_sem.at[to],
-            recv_sem=brecv_sem.at[frm], device_id={"gy": to}, device_id_type=MESH)
-
-    def local_group(i, _):
+            src_ref=b_send.at[to], dst_ref=edge.at[owner], send_sem=bsend_sem.at[to],
+            recv_sem=erecv_sem.at[owner], device_id={"gy": 2 * to + core}, device_id_type=MESH)
+
+    def r_copy(owner):
+        return pltpu.make_async_remote_copy(
+            src_ref=edge.at[owner], dst_ref=edge.at[owner], send_sem=rsend_sem.at[owner // 2],
+            recv_sem=erecv_sem.at[owner], device_id={"gy": sibling}, device_id_type=MESH)
+
+    def local_group(i):
         g = nearest(groups - 1 - i, me // group, groups)
         load(i).wait()
         part = pl.ds(pl.multiple_of(g * count, count), count)
@@ -133,30 +148,58 @@
                         sums[p] = sums[p] + (theta * e[p] - src)
                     e_buf[p, q, j, part] = e[p]
                 if j == last:
+                    end, beta = right, right
                     carry = ls
-                    theta = 1.0 + ls
+                    tau = ls
                 else:
+                    end = end + carry * right
+                    beta = beta + theta * right
                     carry = carry * ls
-                    theta = 1.0 + ls * theta
+                    tau = ls * theta
+                theta = 1.0 + tau
+            for k, value in enumerate((*e, *yl, *sums, ls, right, carry, end, tau, beta)):
+                for m in range(group):
+                    both[core, g * group + m, k, q] = value[m * per:(m + 1) * per]
+
+        @pl.when(i == 0)
+        def _():
+            pl.semaphore_wait(barrier, n + nk - 2)
+
+        d_copy(core, g).start()
+
+    def combine_group(i):
+        g = nearest(groups - 1 - i, me // group, groups)
+        d_copy(1 - core, g).wait_recv()
+        for m in range(group // 2):
+            to = g * (group // 2) + m
+            chunk = 2 * to + core
+            low = [both[0, chunk, k] for k in range(12)]
+            high = [both[1, chunk, k] for k in range(12)]
+            inv = 1.0 / (1.0 - low[9] * high[6])
             for p in range(2):
-                for k, value in enumerate((e[p], yl[p], sums[p])):
-                    for m in range(group):
-                        y_send[g * group + m, k, p, q] = value[m * per:(m + 1) * per]
-
-        @pl.when(i == 0)
-        def _():
-            pl.semaphore_wait(barrier, n + nk - 2)
-
-        for m in range(group):
-            to = g * group + m
-
-            @pl.when(to != me)
+                below = inv * (low[2 + p] + low[9] * high[p])
+                above = high[p] + high[6] * below
+                y_send[to, 0, p] = low[p] + low[7] * above
+                y_send[to, 1, p] = high[2 + p] + high[8] * below
+                y_send[to, 2, p] = (low[4 + p] + high[4 + p]) + (low[11] * above + high[10] * below)
+
+            @pl.when(to != chip)
             def _():
-                y_copy(to, me).start()
-        return 0
-
-    lax.fori_loop(0, groups, local_group, 0)
-    y_recv[me] = y_send[me]
+                y_copy(to, chip).start()
+
+    def up_phase(i, _):
+        @pl.when(i < groups)
+        def _():
+            local_group(i)
+
+        @pl.when(i > 0)
+        def _():
+            combine_group(i - 1)
+
+        return 0
+
+    lax.fori_loop(0, groups + 1, up_phase, 0)
+    y_recv[chip] = y_send[chip]
 
     lam = shift_of(ka * pairs + me * (per * LANES), per)
     lam2 = lam * lam
@@ -188,18 +231,32 @@
 
     lax.fori_loop(0, n // unroll, responses, 0)
 
+    def chip_responses(c, _):
+        a0, b0, c0, d0, alpha0, beta0 = (coef[2 * c, k] for k in range(6))
+        a1, b1, c1, d1, alpha1, beta1 = (coef[2 * c + 1, k] for k in range(6))
+        inv = 1.0 / (1.0 - d0 * a1)
+        low_left, low_right = inv * c0, inv * d0 * b1
+        high_left, high_right = a1 * low_left, b1 * inv
+        for k, value in enumerate((a0 + b0 * high_left, b0 * high_right, c1 * low_left, d1 + c1 * low_right,
+                                   alpha0 + beta0 * high_left + alpha1 * low_left,
+                                   beta1 + beta0 * high_right + alpha1 * low_right)):
+            coef[c, k] = value
+        return 0
+
+    lax.fori_loop(0, chips, chip_responses, 0)
+
     def y_arrived(k, _):
-        y_copy(me, lax.rem(me + k, n)).wait_recv()
-        return 0
-
-    lax.fori_loop(1, n, y_arrived, 0)
+        y_copy(chip, lax.rem(chip + k, chips)).wait_recv()
+        return 0
+
+    lax.fori_loop(1, chips, y_arrived, 0)
 
     zero = jnp.zeros((2, per, LANES), jnp.float32)
     for k in range(3):
-        elim[n, k] = zero
+        elim[chips, k] = zero
 
     def up_sweep(k, state):
-        g = n - 1 - k
+        g = chips - 1 - k
         f0, f1, phi, s0, s1, psi = state
         a, b, c, d, alpha, beta = (coef[g, m] for m in range(6))
         inv = 1.0 / (1.0 - d * phi)
@@ -218,7 +275,7 @@
         elim[g, 5] = lamb
         return new_f[0], new_f[1], new_phi, new_s[0], new_s[1], new_psi
 
-    state = lax.fori_loop(0, n, up_sweep, (zero,) * 6)
+    state = lax.fori_loop(0, chips, up_sweep, (zero,) * 6)
     wall = 1.0 / state[5]
 
     def down_sweep(g, left):
@@ -228,32 +285,47 @@
         for p in range(2):
             b_send[g, 1, p] = elim[g + 1, p] + elim[g + 1, 2] * new[p]
 
-        @pl.when(g != me)
+        @pl.when(g != chip)
         def _():
             b_copy(g, me).start()
 
         return new[0], new[1]
 
-    lax.fori_loop(0, n, down_sweep, (-state[3] * wall, -state[4] * wall))
-    b_recv[me] = b_send[me]
+    lax.fori_loop(0, chips, down_sweep, (-state[3] * wall, -state[4] * wall))
+    edge[me] = b_send[chip]
     sq_buf[...] = jnp.zeros_like(sq_buf)
 
-    def close_group(i, _):
+    def relay_group(i):
         g = nearest(i, me // group, groups)
-        for m in range(group):
-            frm = g * group + m
-
-            @pl.when(frm != me)
+        for m in range(group // 2):
+            owner = g * group + 2 * m + core
+
+            @pl.when(owner != me)
             def _():
-                b_copy(me, frm).wait_recv()
-
+                b_copy(chip, owner).wait_recv()
+
+            r_copy(owner).start()
+
+    def close_group(i):
+        g = nearest(i, me // group, groups)
+        for m in range(group // 2):
+            r_copy(g * group + 2 * m + 1 - core).wait_recv()
         part = pl.ds(pl.multiple_of(g * count, count), count)
         lam = shift_of(ka * pairs + g * (count * LANES), count)
         kappa = viscous_rate / lam
-        joined = lambda k, p, q: jnp.concatenate([b_recv[g * group + m, k, p, q] for m in range(group)], axis=0)
+        joined = lambda get: jnp.concatenate([get(g * group + m) for m in range(group)], axis=0)
         for q in range(2):
-            z = [joined(0, p, q) for p in range(2)]
-            after = [joined(1, p, q) for p in range(2)]
+            low = [joined(lambda c: both[0, c, k, q]) for k in range(12)]
+            high = [joined(lambda c: both[1, c, k, q]) for k in range(12)]
+            inv = 1.0 / (1.0 - low[9] * high[6])
+            z, after = [], []
+            for p in range(2):
+                outer_left = joined(lambda c: edge[c, 0, p, q])
+                outer_right = joined(lambda c: edge[c, 1, p, q])
+                below = inv * (low[2 + p] + low[9] * (high[p] + high[7] * outer_right) + low[8] * outer_left)
+                above = high[p] + high[6] * below + high[7] * outer_right
+                z.append(jnp.where(core == 0, outer_left, below))
+                after.append(jnp.where(core == 0, above, outer_right))
             for j in range(rows):
                 ls = ls_buf[q, j, part]
                 right = r_buf[q, j, part]
@@ -266,9 +338,19 @@
                     square = x * x if p == 0 else square + x * x
                 sq_buf[q, j] += sum(square[m * per:(m + 1) * per] for m in range(group))
         store(i).start()
-        return 0
-
-    lax.fori_loop(0, groups, close_group, 0)
+
+    def down_phase(i, _):
+        @pl.when(i < groups)
+        def _():
+            relay_group(i)
+
+        @pl.when(i > 0)
+        def _():
+            close_group(i - 1)
+
+        return 0
+
+    lax.fori_loop(0, groups + 1, down_phase, 0)
 
     mine[...] = jnp.sum(sq_buf[...], axis=2)
 
@@ -281,12 +363,24 @@
         s_copy(k).start()
 
     def sent(k, _):
-        to = lax.rem(me + k, n)
-        y_copy(to, me).wait_send()
+        to = lax.rem(chip + k, chips)
+        y_copy(to, chip).wait_send()
         b_copy(to, me).wait_send()
         return 0
 
-    lax.fori_loop(1, n, sent, 0)
+    lax.fori_loop(1, chips, sent, 0)
+
+    def relayed(c, _):
+        r_copy(2 * c + core).wait_send()
+        return 0
+
+    lax.fori_loop(0, chips, relayed, 0)
+
+    def given(g, _):
+        d_copy(core, g).wait_send()
+        return 0
+
+    lax.fori_loop(0, groups, given, 0)
     added = mine[...]
     for k in range(1, nk):
         s_copy(k).wait_recv()
@@ -307,6 +401,7 @@
     per = pairs // (LANES * n)
     tile = 8 if rows % 8 == 0 else 1
     cols = pairs // LANES
+    chips = n // 2
     group = next((g for g in range(2, n) if n % g == 0 and g * per * tile % 8 == 0), n)
     span = group * per * tile
     f = jnp.transpose(driving_coefficients, (0, 2, 3, 1)).reshape(2, 2, rows // tile, tile, cols, LANES)
@@ -327,20 +422,19 @@
             pltpu.VMEM((2, rows, cols, LANES), f32),
             pltpu.VMEM((2, rows, cols, LANES), f32),
             pltpu.VMEM((2, rows, per, LANES), f32),
-            pltpu.VMEM((n, 3, 2, 2, per, LANES), f32),
-            pltpu.VMEM((n, 3, 2, 2, per, LANES), f32),
+            pltpu.VMEM((2, n, 12, 2, per, LANES), f32),
+            pltpu.VMEM((chips, 3, 2, 2, per, LANES), f32),
+            pltpu.VMEM((chips, 3, 2, 2, per, LANES), f32),
             pltpu.VMEM((n, 6, 2, per, LANES), f32),
-            pltpu.VMEM((n + 1, 6, 2, per, LANES), f32),
-            pltpu.VMEM((n, 2, 2, 2, per, LANES), f32),
+            pltpu.VMEM((chips + 1, 6, 2, per, LANES), f32),
+            pltpu.VMEM((chips, 2, 2, 2, per, LANES), f32),
             pltpu.VMEM((n, 2, 2, 2, per, LANES), f32),
             pltpu.VMEM((2, rows, LANES), f32),
             pltpu.VMEM((nk - 1, 2, rows, LANES), f32),
-            pltpu.SemaphoreType.DMA((n // group,)),
-            pltpu.SemaphoreType.DMA((n // group,)),
+            *[pltpu.SemaphoreType.DMA((n // group,))] * 4,
+            *[pltpu.SemaphoreType.DMA((chips,))] * 3,
             pltpu.SemaphoreType.DMA((n,)),
-            pltpu.SemaphoreType.DMA((n,)),
-            pltpu.SemaphoreType.DMA((n,)),
-            pltpu.SemaphoreType.DMA((n,)),
+            pltpu.SemaphoreType.DMA((chips,)),
             pltpu.SemaphoreType.DMA((nk - 1,)),
             pltpu.SemaphoreType.DMA((nk - 1,)),
         ],

time: 31.3 us -> 29 us (0.927)
  Pallas kernels: 26.1 us -> 23.8 us
    pallas_call x1, Pallas kernels: 26.1 us -> 23.8 us  [per_device(): pl.pallas_call(functools.partial(channel_kernel, n, nk, per, rows, tile,...]
where the time goes in v3:
time: 29 us; the launch traced here: 28.8 us
  Pallas kernels  23.8 us (82%)
  local copies, waits for them, and re-layouts  4.32 us (15%)
  between operations  0.65 us (2%)
    pallas_call x1, Pallas kernels, per_device(): pl.pallas_call(functools.partial(channel_kernel, n, nk, per, rows, tile,...  23.8 us
    unnamed x4, local copies, waits for them, and re-layouts  4.32 us

profile of v3, /device:TPU:0, one launch (start us, length us, event | category | flops | bytes accessed | tf_op | source)
XLA Modules:
  0.0 28.8 jit_solution(8609005035161010512)
XLA Ops:
  0.6 23.8 %channel_substep.1 = (f32[2,2,3,512,128]{4,3,2,1,0:T(8,128)}, f32[2,24]{1,0:T(2,128)}) custom-call(f32[1536]{0:T(1024)} %constant.2.clone.w_ref, f32[2,2,3,512,128]{4,3,2,1,0:T(8,128)} %bitcast.14), custom_call_target="tpu_custom_call" | custom-call | tf_op jit(solution)/shard_map/channel_substep/pallas_call | solution.py:413
  24.4 0.0 copy-start
  24.4 3.8 %copy.6 = f32[2,8192,2,24]{1,3,2,0:T(8,128)} copy(f32[2,8192,2,24]{1,3,2,0:T(8,128)} %bitcast.15) | data formatting | bytes 6291456
  28.2 0.0 copy-done
  28.2 0.6 %copy.7 = f32[2,24]{1,0:T(2,128)} copy(f32[2,24]{1,0:T(2,128)S(1)} %copy-done) | data formatting | bytes 384
Async XLA Ops:
  24.4 3.8 %copy-start = (f32[2,24]{1,0:T(2,128)S(1)}, f32[2,24]{1,0:T(2,128)}, u32[]{:S(2)}) copy-start(f32[2,24]{1,0:T(2,128)} %get-tuple-element.9) | copy-start | bytes 580

commit v4 on v3

--- a/solution.py
+++ b/solution.py
@@ -54,9 +54,9 @@
     return s, low * s, lam * at(2)
 
 
-def channel_kernel(n, nk, per, rows, tile, group, scale, w_ref, f_hbm, x_hbm, spec_ref,
-                   f_buf, x_buf, e_buf, ls_buf, r_buf, sq_buf, both, y_send, y_recv, coef, elim, b_send, edge, mine, held,
-                   load_sem, store_sem, dsend_sem, drecv_sem, ysend_sem, yrecv_sem, bsend_sem, erecv_sem, rsend_sem,
+def channel_kernel(n, nk, per, rows, tile, group, scale, w_hbm, f_hbm, x_buf, spec_ref,
+                   w_ref, f_buf, e_buf, ls_buf, r_buf, sq_buf, both, y_send, y_recv, coef, elim, b_send, edge, mine, held,
+                   table_sem, load_sem, dsend_sem, drecv_sem, ysend_sem, yrecv_sem, bsend_sem, erecv_sem, rsend_sem,
                    ssend_sem, srecv_sem):
     total = n * rows
     last = rows - 1
@@ -78,11 +78,8 @@
         where = pl.ds(pl.multiple_of(g * span, span), span)
         return pltpu.make_async_copy(f_hbm.at[:, :, :, where, :], f_buf.at[:, :, :, where, :], load_sem.at[i])
 
-    def store(i):
-        g = nearest(i, me // group, groups)
-        where = pl.ds(pl.multiple_of(g * span, span), span)
-        return pltpu.make_async_copy(x_buf.at[:, :, :, where, :], x_hbm.at[:, :, :, where, :], store_sem.at[i])
-
+    table = pltpu.make_async_copy(w_hbm, w_ref, table_sem)
+    table.start()
     for i in range(groups):
         load(i).start()
 
@@ -187,6 +184,8 @@
             def _():
                 y_copy(to, chip).start()
 
+    table.wait()
+
     def up_phase(i, _):
         @pl.when(i < groups)
         def _():
@@ -337,7 +336,6 @@
                     x_buf[where] = x
                     square = x * x if p == 0 else square + x * x
                 sq_buf[q, j] += sum(square[m * per:(m + 1) * per] for m in range(group))
-        store(i).start()
 
     def down_phase(i, _):
         @pl.when(i < groups)
@@ -392,8 +390,6 @@
         spec_ref[q:q + 1, :] = sums[0:1] * scale
     for k in range(1, nk):
         s_copy(k).wait_send()
-    for i in range(groups):
-        store(i).wait()
 
 
 def per_device(n, nk, driving_coefficients):
@@ -407,16 +403,15 @@
     f = jnp.transpose(driving_coefficients, (0, 2, 3, 1)).reshape(2, 2, rows // tile, tile, cols, LANES)
     f = jnp.swapaxes(f, 3, 4).reshape(2, 2, rows // tile, cols * tile, LANES)
     table = jnp.asarray(weight_table(n * rows))
-    smem = pl.BlockSpec(memory_space=pltpu.SMEM)
     vmem = pl.BlockSpec(memory_space=pltpu.VMEM)
     f32 = jnp.float32
     x, spectrum = pl.pallas_call(
         functools.partial(channel_kernel, n, nk, per, rows, tile, group, 1.0 / (2.0 * pairs * nk)),
         out_shape=(jax.ShapeDtypeStruct(f.shape, f32), jax.ShapeDtypeStruct((2, rows), f32)),
-        in_specs=[smem, pl.BlockSpec(memory_space=pl.ANY)],
-        out_specs=(pl.BlockSpec(memory_space=pl.ANY), vmem),
+        in_specs=[pl.BlockSpec(memory_space=pltpu.HBM)] * 2,
+        out_specs=(vmem, vmem),
         scratch_shapes=[
-            pltpu.VMEM(f.shape, f32),
+            pltpu.SMEM(table.shape, f32),
             pltpu.VMEM(f.shape, f32),
             pltpu.VMEM((2, 2, rows, cols, LANES), f32),
             pltpu.VMEM((2, rows, cols, LANES), f32),
@@ -431,16 +426,17 @@
             pltpu.VMEM((n, 2, 2, 2, per, LANES), f32),
             pltpu.VMEM((2, rows, LANES), f32),
             pltpu.VMEM((nk - 1, 2, rows, LANES), f32),
-            *[pltpu.SemaphoreType.DMA((n // group,))] * 4,
+            pltpu.SemaphoreType.DMA,
+            *[pltpu.SemaphoreType.DMA((n // group,))] * 3,
             *[pltpu.SemaphoreType.DMA((chips,))] * 3,
             pltpu.SemaphoreType.DMA((n,)),
             pltpu.SemaphoreType.DMA((chips,)),
             pltpu.SemaphoreType.DMA((nk - 1,)),
             pltpu.SemaphoreType.DMA((nk - 1,)),
         ],
-        compiler_params=pltpu.CompilerParams(collective_id=0, has_side_effects=True),
+        compiler_params=pltpu.CompilerParams(collective_id=0, has_side_effects=True, vmem_limit_bytes=24 << 20),
         name="channel_substep",
-    )(table, f)
+    )(*(pltpu.with_memory_space_constraint(given, pltpu.HBM) for given in (table, f)))
     x = jnp.swapaxes(x.reshape(2, 2, rows // tile, cols, tile, LANES), 3, 4).reshape(2, 2, rows, pairs)
     return jnp.transpose(x, (0, 3, 1, 2)), spectrum
 

time: 29 us -> 25.3 us (0.87)
  local copies, waits for them, and re-layouts: 4.32 us -> 2.23 us
  Pallas kernels: 23.8 us -> 22.3 us
    unnamed x4 -> x2, local copies, waits for them, and re-layouts: 4.32 us -> 2.23 us
    pallas_call x1, Pallas kernels: 23.8 us -> 22.3 us  [per_device(): pl.pallas_call(functools.partial(channel_kernel, n, nk, per, rows, tile,...]
where the time goes in v4:
time: 25.3 us; the launch traced here: 25.1 us
  Pallas kernels  22.3 us (88%)
  local copies, waits for them, and re-layouts  2.23 us (9%)
  between operations  0.64 us (3%)
    pallas_call x1, Pallas kernels, per_device(): pl.pallas_call(functools.partial(channel_kernel, n, nk, per, rows, tile,...  22.3 us
    unnamed x2, local copies, waits for them, and re-layouts  2.23 us

profile of v4, /device:TPU:0, one launch (start us, length us, event | category | flops | bytes accessed | tf_op | source)
XLA Modules:
  0.0 25.1 jit_solution(13068656664512028631)
XLA Ops:
  0.6 22.3 %channel_substep.1 = (f32[2,2,3,512,128]{4,3,2,1,0:T(8,128)S(1)}, f32[2,24]{1,0:T(2,128)S(1)}) custom-call(f32[1536]{0:T(1024)} %constant.2.clone.w_hbm, f32[2,2,3,512,128]{4,3,2,1,0:T(8,128)} %bitcast.15), custom_call_target="tpu_custom_call" | custom-call | tf_op jit(solution)/shard_map/channel_substep/pallas_call | solution.py:408
  22.9 1.7 %copy.6 = f32[2,8192,2,24]{1,3,2,0:T(8,128)} copy(f32[2,8192,2,24]{1,3,2,0:T(8,128)S(1)} %bitcast.14) | data formatting | bytes 6291456
  24.6 0.6 %copy.7 = f32[2,24]{1,0:T(2,128)} copy(f32[2,24]{1,0:T(2,128)S(1)} %get-tuple-element.9) | data formatting | bytes 384

commit v5 on v4

--- a/solution.py
+++ b/solution.py
@@ -242,7 +242,7 @@
             coef[c, k] = value
         return 0
 
-    lax.fori_loop(0, chips, chip_responses, 0)
+    lax.fori_loop(0, chips, chip_responses, 0, unroll=chips <= 8)
 
     def y_arrived(k, _):
         y_copy(chip, lax.rem(chip + k, chips)).wait_recv()
@@ -274,7 +274,7 @@
         elim[g, 5] = lamb
         return new_f[0], new_f[1], new_phi, new_s[0], new_s[1], new_psi
 
-    state = lax.fori_loop(0, chips, up_sweep, (zero,) * 6)
+    state = lax.fori_loop(0, chips, up_sweep, (zero,) * 6, unroll=chips <= 8)
     wall = 1.0 / state[5]
 
     def down_sweep(g, left):
@@ -290,7 +290,7 @@
 
         return new[0], new[1]
 
-    lax.fori_loop(0, chips, down_sweep, (-state[3] * wall, -state[4] * wall))
+    lax.fori_loop(0, chips, down_sweep, (-state[3] * wall, -state[4] * wall), unroll=chips <= 8)
     edge[me] = b_send[chip]
     sq_buf[...] = jnp.zeros_like(sq_buf)
 

time: 25.3 us -> 25.3 us (level)
  no operation moved by 1% of the time
where the time goes in v5:
time: 25.3 us; the launch traced here: 25.1 us
  Pallas kernels  22.3 us (88%)
  local copies, waits for them, and re-layouts  2.23 us (9%)
  between operations  0.64 us (3%)
    pallas_call x1, Pallas kernels, per_device(): pl.pallas_call(functools.partial(channel_kernel, n, nk, per, rows, tile,...  22.3 us
    unnamed x2, local copies, waits for them, and re-layouts  2.23 us

profile of v5, /device:TPU:0, one launch (start us, length us, event | category | flops | bytes accessed | tf_op | source)
XLA Modules:
  0.0 25.1 jit_solution(9693418967869708025)
XLA Ops:
  0.6 22.3 %channel_substep.1 = (f32[2,2,3,512,128]{4,3,2,1,0:T(8,128)S(1)}, f32[2,24]{1,0:T(2,128)S(1)}) custom-call(f32[1536]{0:T(1024)} %constant.2.clone.w_hbm, f32[2,2,3,512,128]{4,3,2,1,0:T(8,128)} %bitcast.15), custom_call_target="tpu_custom_call" | custom-call | tf_op jit(solution)/shard_map/channel_substep/pallas_call | solution.py:408
  22.9 1.7 %copy.6 = f32[2,8192,2,24]{1,3,2,0:T(8,128)} copy(f32[2,8192,2,24]{1,3,2,0:T(8,128)S(1)} %bitcast.14) | data formatting | bytes 6291456
  24.6 0.6 %copy.7 = f32[2,24]{1,0:T(2,128)} copy(f32[2,24]{1,0:T(2,128)S(1)} %get-tuple-element.9) | data formatting | bytes 384
